TPU v7x, 32 devices: a whole 2x2x4 slice. The times are simulated.
32 devices in a mesh: layer: 4 (over y, core), col: 4 (over z), row: 2 (over x).
Axes of the slice: x: 2, y: 2, z: 4, core: 2. Of those that a mesh axis runs over, the one named last changes fastest.
Arguments:
- activations: bfloat16 [4, 768, 4096], P(None, ('layer', 'row'), 'col'), may hold values from -6 to 6
- out_grads: bfloat16 [4, 768, 11008], P(None, ('layer', 'col'), 'row'), may hold values from -0.02734375 to 0.02734375
- basis_in: bfloat16 [4, 4096, 4096], P('layer', 'col', 'row'), may hold values from -0.09375 to 0.09375
- basis_out: bfloat16 [4, 11008, 11008], P('layer', 'row', 'col'), may hold values from -0.0546875 to 0.0546875
- eigenvalues: float32 [4, 11008, 4096], P('layer', 'col', 'row'), may hold values from 0.01 to 10
- damping: float32 [4], P('layer'), may hold values from 0.05 to 0.5
- layer_order: int32 [4], replicated, may hold values from 0 to 3, each once
- query_ids: int32 [256], replicated, may hold values from 0 to 3, never falling along the last dimension, each value on 1 to 128 neighbouring positions
- train_ids: int32 [512], replicated, may hold values from 0 to 15, never falling along the last dimension, each value on 1 to 64 neighbouring positions
Outputs:
- scores: float32 [4, 16], replicated
Inputs may be any that keep to these rules, and one draw needn't show every extreme that they name: `layer_order`: each slot's layer appears once. `query_ids`: never falling; every query example has 1 to 128 tokens. `train_ids`: never falling; every train example has 1 to 64 tokens.
All inputs are finite; a program needn't handle non-finite values.
Results may differ from a plain program's by a relative error of at most 0.02.
Values may be sent and summed in bfloat16 or wider, within the bound.
No kernel may reach another device: no remote copies, remote signals or barrier semaphores. Data moves between devices by JAX's collectives and lax.ppermute only.
A program may use at most 192 MiB of HBM per device.

v0:
```python
import jax
import jax.numpy as jnp
from jax import lax
from jax.sharding import PartitionSpec as P

QUERIES = 4
TRAIN = 16


def body(
    activations,
    out_grads,
    basis_in,
    basis_out,
    eigenvalues,
    damping,
    layer_order,
    query_ids,
    train_ids,
):
    slot_count = basis_in.shape[0]
    layer_groups = lax.axis_size("layer")
    row_count = lax.axis_size("row")
    col_count = lax.axis_size("col")
    ordered_in = jnp.take(activations, layer_order, axis=0)
    ordered_out = jnp.take(out_grads, layer_order, axis=0)
    in_block = ordered_in.shape[1]
    moved_in = lax.all_to_all(ordered_in, "layer", split_axis=0, concat_axis=1, tiled=True)
    shaped_in = moved_in.reshape(slot_count, layer_groups, in_block, moved_in.shape[2])
    joined_in = lax.all_gather(shaped_in, "row", axis=2, tiled=True)
    inputs_full = joined_in.reshape(
        slot_count, layer_groups * row_count * in_block, moved_in.shape[2]
    )
    out_block = ordered_out.shape[1]
    moved_out = lax.all_to_all(ordered_out, "layer", split_axis=0, concat_axis=1, tiled=True)
    shaped_out = moved_out.reshape(slot_count, layer_groups, out_block, moved_out.shape[2])
    joined_out = lax.all_gather(shaped_out, "col", axis=2, tiled=True)
    grads_full = joined_out.reshape(
        slot_count, layer_groups * col_count * out_block, moved_out.shape[2]
    )
    partial_in = jnp.einsum(
        "ltc,lcj->ltj", inputs_full, basis_in, preferred_element_type=jnp.float32
    )
    rotated_in = lax.psum(partial_in.astype(jnp.bfloat16), "col")
    partial_out = jnp.einsum(
        "ltr,lri->lti", grads_full, basis_out, preferred_element_type=jnp.float32
    )
    rotated_out = lax.psum(partial_out.astype(jnp.bfloat16), "row")
    query_tokens = query_ids.shape[0]
    query_mask = (query_ids[None, :] == jnp.arange(QUERIES, dtype=jnp.int32)[:, None]).astype(
        jnp.bfloat16
    )
    train_onehot = (train_ids[:, None] == jnp.arange(TRAIN, dtype=jnp.int32)[None, :]).astype(
        jnp.float32
    )
    query_in = rotated_in[0, :query_tokens]
    query_out = rotated_out[0, :query_tokens]
    train_in = rotated_in[0, query_tokens:]
    train_out = rotated_out[0, query_tokens:]
    masked = query_mask[:, :, None] * query_in[None, :, :]
    query_gram = jnp.einsum("si,qsj->qij", query_out, masked, preferred_element_type=jnp.float32)
    precond = (query_gram / (eigenvalues[0] + damping[0])).astype(jnp.bfloat16)
    mapped = jnp.einsum("ui,qij->quj", train_out, precond, preferred_element_type=jnp.float32)
    values = jnp.sum(mapped * train_in[None, :, :], axis=2)
    total = jnp.dot(values, train_onehot, precision=lax.Precision.HIGHEST)
    return lax.psum(total, ("layer", "col", "row"))


def solution(mesh):
    in_specs = (
        P(None, ("layer", "row"), "col"),
        P(None, ("layer", "col"), "row"),
        P("layer", "col", "row"),
        P("layer", "row", "col"),
        P("layer", "col", "row"),
        P("layer"),
        P(),
        P(),
        P(),
    )
    out_specs = P()
    return jax.shard_map(body, mesh=mesh, in_specs=in_specs, out_specs=out_specs, check_vma=False)
```

profile of v0, /device:TPU:0, one launch (start us, length us, event | category | flops | bytes accessed | tf_op | source)
XLA Modules:
  0.0 537.3 jit_solution(4422896807830578401)
XLA Ops:
  6.5 0.0 copy-start
  6.5 0.8 compare_and_fusion
  7.3 0.7 compare_select_fusion
  8.0 1.7 gather_fusion
  9.8 1.0 broadcast_select_fusion.1
  10.8 4.3 all-to-all-start
  15.0 0.0 copy-done
  15.0 2.1 gather_fusion.1
  17.1 3.2 broadcast_select_fusion
  20.3 6.3 %all-to-all-done = bf16[4,96,1024]{2,1,0:T(8,128)(2,1)S(1)} async-done(((bf16[4,96,1024]{2,1,0:T(8,128)(2,1)}), bf16[4,96,1024]{2,1,0:T(8,128)(2,1)S(1)}, u32[]{:S(2)}, u32[]{:S(2)}) %all-to-all-start) | async-done | bytes 786464 | tf_op jit(solution)/shard_map/all_to_all | solution.py:28
  26.7 0.0 copy-start.3
  26.7 3.6 all-to-all-start.1
  30.3 0.0 all-gather.5.cloned.1.call-start
  30.3 0.0 copy-done.3
  30.3 0.7 all-gather.5.cloned.1.call-update
  31.0 0.0 all-gather.7.cloned.1.call-start
  31.1 25.0 %all-to-all-done.1 = bf16[4,48,5504]{2,1,0:T(8,128)(2,1)S(1)} async-done(((bf16[4,48,5504]{2,1,0:T(8,128)(2,1)}), bf16[4,48,5504]{2,1,0:T(8,128)(2,1)S(1)}, u32[]{:S(2)}, u32[]{:S(2)}) %all-to-all-start.1) | async-done | bytes 2113568 | tf_op jit(solution)/shard_map/all_to_all | solution.py:35
  56.1 0.0 copy-start.2
  56.1 1.3 copy-done.2
  57.4 0.0 all-gather.7.cloned.1.call-update
  57.5 0.0 all-reduce.3.cloned.1.call-start
  57.5 4.7 all-gather.5.cloned.1.call-done
  62.2 7.7 %fusion.18 = bf16[1,768,2048]{2,1,0:T(8,128)(2,1)} fusion(bf16[768,1024]{1,0:T(8,128)(2,1)} %bitcast.69, bf16[1,1024,2048]{2,1,0:T(8,128)(2,1)} %param.11), kind=kOutput, calls=%fused_computation.16 | convolution fusion | flops 3222798336 | bytes 8912896 | tf_op jit(solution)/shard_map/ltc,lcj->ltj/dot_general | solution.py:41
  70.0 0.0 all-reduce.3.cloned.1.call-update
  70.0 0.2 all-reduce.5.cloned.1.call-start
  70.2 144.3 %all-gather.7.cloned.1.call-done = bf16[4,192,5504]{2,1,0:T(8,128)(2,1)} async-done(((bf16[4,48,5504]{2,1,0:T(8,128)(2,1)}), bf16[4,192,5504]{2,1,0:T(8,128)(2,1)}) %all-gather.7.cloned.1.call-update) | async-done | bytes 8454160 | tf_op jit(solution)/shard_map/all_gather | solution.py:37
  214.5 31.3 %fusion.8 = bf16[1,768,2752]{1,2,0:T(8,128)(2,1)} fusion(bf16[768,5504]{1,0:T(8,128)(2,1)} %bitcast.68, bf16[1,5504,2752]{1,2,0:T(8,128)(2,1)} %param.12), kind=kOutput, calls=%fused_computation.11 | convolution fusion | flops 23267917824 | bytes 42975232 | tf_op jit(solution)/shard_map/ltr,lri->lti/dot_general | solution.py:45
  245.8 0.0 copy-start.4
  245.8 0.0 all-reduce.5.cloned.1.call-update
  246.5 0.0 copy-done.4
  246.5 17.0 %add_bitcast_fusion = f32[2752,2048]{1,0:T(8,128)} fusion(f32[1,2752,2048]{2,1,0:T(8,128)} %param.13, f32[]{:T(128)} %bitcast.67), kind=kLoop, calls=%fused_computation.7 | loop fusion | flops 5636096 | bytes 45088772 | tf_op jit(solution)/shard_map/div | solution.py:62
  263.5 72.7 %all-reduce.3.cloned.1.call-done = bf16[1,768,2048]{2,1,0:T(8,128)(2,1)} async-done(((bf16[1,768,2048]{2,1,0:T(8,128)(2,1)}), bf16[1,768,2048]{2,1,0:T(8,128)(2,1)}) %all-reduce.3.cloned.1.call-update) | async-done | bytes 3145744 | tf_op jit(solution)/shard_map/psum | solution.py:44
  336.2 4.1 fusion.21
  340.2 5.4 %copy.12 = f32[512,2048]{0,1:T(8,128)} copy(f32[512,2048]{1,0:T(8,128)} %fusion.21) | data formatting | bytes 8388608 | tf_op jit(solution)/shard_map/mul | solution.py:64
  345.7 1.3 slice_bitcast_fusion.6
  347.0 99.2 %all-reduce.5.cloned.1.call-done = bf16[1,768,2752]{1,2,0:T(8,128)(2,1)} async-done(((bf16[1,768,2752]{1,2,0:T(8,128)(2,1)}), bf16[1,768,2752]{1,2,0:T(8,128)(2,1)}) %all-reduce.5.cloned.1.call-update) | async-done | bytes 4227088 | tf_op jit(solution)/shard_map/psum | solution.py:48
  446.1 3.6 slice_bitcast_fusion.13
  449.7 0.0 copy-start.5
  449.7 0.0 copy-start.1
  449.7 41.4 %fusion.4 = f32[4,512]{1,0:T(4,128)S(1)} fusion(f32[512,2048]{0,1:T(8,128)} %copy.12, f32[2752,2048]{1,0:T(8,128)} %add_bitcast_fusion, bf16[1,768,2752]{1,2,0:T(8,128)(2,1)} %all-reduce.5.cloned.1.call-done, bf16[256,2048]{1,0:T(8,128)(2,1)S(1)} %slice_bitcast_fusion.6, bf16[4,256]{1,0:T(4,128)(2,1)S(1)} %fusion.28, ...), kind=kOutput, calls=%fused_computation.9 | convolution fusion | flops 34690039808 | bytes 32024576 | tf_op jit(solution)/shard_map/ui,qij->quj/dot_general | solution.py:63
  491.1 0.0 copy-done.5
  491.2 0.3 fusion.26
  491.4 39.3 %psum.23 = f32[4,16]{1,0:T(4,128)} all-reduce(f32[4,16]{1,0:T(4,128)S(1)} %fusion.26), channel_id=1, replica_groups=mesh['layer'=4,'col'=4,'row'=2] {'layer','col','row'}, use_global_device_ids=true, to_apply=%region_3.4 | all-reduce | flops 64 | bytes 512 | tf_op jit(solution)/shard_map/psum | solution.py:66
  530.7 0.0 copy-done.1
  (2 shorter events, 0.0 us)
Async XLA Ops:
  6.5 8.5 %copy-start = (bf16[4,48,5504]{2,1,0:T(8,128)(2,1)S(1)}, bf16[4,48,5504]{2,1,0:T(8,128)(2,1)}, u32[]{:S(2)}) copy-start(bf16[4,48,5504]{2,1,0:T(8,128)(2,1)} %param.10) | copy-start | bytes 6340612
  10.8 15.9 %all-to-all-start = ((bf16[4,96,1024]{2,1,0:T(8,128)(2,1)}), bf16[4,96,1024]{2,1,0:T(8,128)(2,1)S(1)}, u32[]{:S(2)}, u32[]{:S(2)}) async-start(bf16[4,96,1024]{2,1,0:T(8,128)(2,1)} %broadcast_select_fusion.1), calls=%async_computation | async-start | bytes 1572864 | tf_op jit(solution)/shard_map/all_to_all | solution.py:28
  26.7 3.7 copy-start.3
  26.7 29.4 %all-to-all-start.1 = ((bf16[4,48,5504]{2,1,0:T(8,128)(2,1)}), bf16[4,48,5504]{2,1,0:T(8,128)(2,1)S(1)}, u32[]{:S(2)}, u32[]{:S(2)}) async-start(bf16[4,48,5504]{2,1,0:T(8,128)(2,1)} %broadcast_select_fusion), calls=%async_computation.1 | async-start | bytes 4227072 | tf_op jit(solution)/shard_map/all_to_all | solution.py:35
  30.3 31.9 %all-gather.5.cloned.1.call-start = ((), (), s32[]{:S(2)}) async-start(), calls=%async_computation.4 | async-start | bytes 2359296 | tf_op jit(solution)/shard_map/all_gather | solution.py:30
  31.0 183.5 %all-gather.7.cloned.1.call-start = ((), (), s32[]{:S(2)}) async-start(), calls=%async_computation.5 | async-start | bytes 10567680 | tf_op jit(solution)/shard_map/all_gather | solution.py:37
  56.1 1.3 copy-start.2
  57.5 278.7 %all-reduce.3.cloned.1.call-start = ((), (), s32[]{:S(2)}) async-start(), calls=%async_computation.2 | async-start | bytes 6291456 | tf_op jit(solution)/shard_map/psum | solution.py:44
  70.0 376.1 %all-reduce.5.cloned.1.call-start = ((), (), s32[]{:S(2)}) async-start(), calls=%async_computation.3 | async-start | bytes 8454144 | tf_op jit(solution)/shard_map/psum | solution.py:48
  245.8 0.7 copy-start.4
  449.7 41.5 %copy-start.5 = (s32[512]{0:T(512)S(1)}, s32[512]{0:T(512)}, u32[]{:S(2)}) copy-start(s32[512]{0:T(512)} %param.17) | copy-start | bytes 6148
  449.7 81.0 %copy-start.1 = (bf16[4,48,5504]{2,1,0:T(8,128)(2,1)S(1)}, bf16[4,48,5504]{2,1,0:T(8,128)(2,1)}, u32[]{:S(2)}) copy-start(bf16[4,48,5504]{2,1,0:T(8,128)(2,1)} %param.10) | copy-start | bytes 6340612
Sparse Core Ops, SparseCore 0:
  32.6 29.5 all-gather.4
  63.8 150.6 all-gather.6
  216.9 119.2 all-reduce.2
  338.5 107.6 all-reduce.4
where the time goes:
time: 538 us; the launch traced here: 537 us
  waiting for transfers between devices  353 us (66%)
  matrix products  80.7 us (15%)
  blocking collectives  39.3 us (7%)
  other arithmetic  26.7 us (5%)
  local copies, waits for them, and re-layouts  15.5 us (3%)
  between operations  13.9 us (3%)
  starting transfers between devices  8.21 us (2%)
    all_gather x1, waiting for transfers between devices, body(): joined_out = lax.all_gather(shaped_out, 'col', axis=2, tiled=True)  144 us
    psum x1, waiting for transfers between devices, body(): rotated_out = lax.psum(partial_out.astype(jnp.bfloat16), 'row')  99.2 us
    psum x1, waiting for transfers between devices, body(): rotated_in = lax.psum(partial_in.astype(jnp.bfloat16), 'col')  72.7 us
    dot_general x1, matrix products, body(): jnp.einsum('ui,qij->quj', train_out, precond, preferred_element_type=jnp....  41.4 us
    psum x1, blocking collectives, body(): return lax.psum(total, ('layer', 'col', 'row'))  39.3 us
    dot_general x1, matrix products, body(): jnp.einsum('ltr,lri->lti', grads_full, basis_out, preferred_element_type=...  31.3 us
    all_to_all x1, waiting for transfers between devices, body(): lax.all_to_all(ordered_out, 'layer', split_axis=0, concat_axis=1, tiled=T...  25 us
    div x1, other arithmetic, body(): precond = (query_gram / (eigenvalues[0] + damping[0])).astype(jnp.bfloat16)  17 us
  transfers between devices with their start and end apart: 6, of which 6 were waited for; matrix products, arithmetic and copies ran while one was open for 13% of the time, Pallas kernels for 0%

commit v1 on v0

--- a/solution.py
+++ b/solution.py
@@ -34,7 +34,12 @@
     out_block = ordered_out.shape[1]
     moved_out = lax.all_to_all(ordered_out, "layer", split_axis=0, concat_axis=1, tiled=True)
     shaped_out = moved_out.reshape(slot_count, layer_groups, out_block, moved_out.shape[2])
-    joined_out = lax.all_gather(shaped_out, "col", axis=2, tiled=True)
+    ring = [shaped_out]
+    for hop in range(3):
+        ring.append(lax.ppermute(ring[-1], "col", [(dev, (dev + 1) % 4) for dev in range(4)]))
+    joined_out = jnp.roll(
+        jnp.concatenate(ring[::-1], axis=2), (lax.axis_index("col") + 1) * ring[0].shape[2], axis=2
+    )
     grads_full = joined_out.reshape(
         slot_count, layer_groups * col_count * out_block, moved_out.shape[2]
     )

time: 538 us -> 502 us (0.933)
  waiting for transfers between devices: 353 us -> 251 us
  blocking collectives: 39.3 us -> 83.9 us
  local copies, waits for them, and re-layouts: 15.5 us -> 45 us
  starting transfers between devices: 8.21 us -> 1.85 us
    ppermute x0 -> x3, waiting for transfers between devices: none -> 154 us  [body(): lax.ppermute(ring[-1], 'col', [(dev, (dev + 1) % 4) for dev in range(4)])]
    all_gather x1 -> x0, waiting for transfers between devices: 144 us -> none  [body(): joined_out = lax.all_gather(shaped_out, 'col', axis=2, tiled=True)]
    psum x1, waiting for transfers between devices: 72.7 us -> 0.01 us  [body(): rotated_in = lax.psum(partial_in.astype(jnp.bfloat16), 'col')]
    all_to_all x0 -> x2, blocking collectives: none -> 44.6 us  [the longest x1 29.9 us: body(): lax.all_to_all(ordered_out, 'layer', split_axis=0, concat_axis=1, tiled=T...]
    all_to_all x2 -> x0, waiting for transfers between devices: 31.3 us -> none  [the longest x1 25 us: body(): lax.all_to_all(ordered_out, 'layer', split_axis=0, concat_axis=1, tiled=T...]
    unnamed x12 -> x15, local copies, waits for them, and re-layouts: 1.36 us -> 19.8 us
    dynamic_slice x0 -> x1, local copies, waits for them, and re-layouts: none -> 9.31 us  [body(): jnp.roll(jnp.concatenate(ring[::-1], axis=2), (lax.axis_index('col') + 1)...]
    all_to_all x2 -> x0, starting transfers between devices: 7.87 us -> none  [the longest x1 4.26 us: body(): lax.all_to_all(ordered_in, 'layer', split_axis=0, concat_axis=1, tiled=True)]
  transfers between devices with their start and end apart: 6 -> 6, of which waited for: 6 -> 4; matrix products, arithmetic and copies ran while one was open for 13% -> 20% of each run, Pallas kernels for 0% -> 0%
where the time goes in v1:
time: 502 us; the launch traced here: 501 us
  waiting for transfers between devices  251 us (50%)
  blocking collectives  83.9 us (17%)
  matrix products  80.8 us (16%)
  local copies, waits for them, and re-layouts  45 us (9%)
  other arithmetic  24.5 us (5%)
  between operations  13.8 us (3%)
    ppermute x3, waiting for transfers between devices, body(): lax.ppermute(ring[-1], 'col', [(dev, (dev + 1) % 4) for dev in range(4)])  154 us
    psum x1, waiting for transfers between devices, body(): rotated_out = lax.psum(partial_out.astype(jnp.bfloat16), 'row')  96.8 us
    dot_general x1, matrix products, body(): jnp.einsum('ui,qij->quj', train_out, precond, preferred_element_type=jnp....  41.4 us
    psum x1, blocking collectives, body(): return lax.psum(total, ('layer', 'col', 'row'))  39.3 us
    dot_general x1, matrix products, body(): jnp.einsum('ltr,lri->lti', grads_full, basis_out, preferred_element_type=...  31.4 us
    all_to_all x1, blocking collectives, body(): lax.all_to_all(ordered_out, 'layer', split_axis=0, concat_axis=1, tiled=T...  29.9 us
    unnamed x15, local copies, waits for them, and re-layouts  19.8 us
    div x1, other arithmetic, body(): precond = (query_gram / (eigenvalues[0] + damping[0])).astype(jnp.bfloat16)  17 us
  transfers between devices with their start and end apart: 6, of which 4 were waited for; matrix products, arithmetic and copies ran while one was open for 20% of the time, Pallas kernels for 0%

profile of v1, /device:TPU:0, one launch (start us, length us, event | category | flops | bytes accessed | tf_op | source)
XLA Modules:
  0.0 501.3 jit_solution(7685259622935953905)
XLA Ops:
  6.5 0.0 copy-start
  6.5 0.0 all-gather.3.cloned.1.call-start
  6.5 0.8 compare_select_fusion
  7.3 0.7 compare_and_fusion
  8.0 0.1 copy-done
  8.1 2.1 gather_fusion.1
  10.2 1.9 broadcast_select_fusion
  12.1 29.9 %all_to_all.8 = bf16[4,48,5504]{2,1,0:T(8,128)(2,1)S(1)} all-to-all(bf16[4,48,5504]{2,1,0:T(8,128)(2,1)S(1)} %broadcast_select_fusion), channel_id=1, replica_groups=mesh['layer'=4,'col'=4,'row'=2] {'layer'}, dimensions={0} | all-to-all | bytes 4227072 | tf_op jit(solution)/shard_map/all_to_all | solution.py:35
  42.0 1.6 collective-permute-start
  43.6 48.3 %collective-permute-done = bf16[1,4,48,5504]{3,2,1,0:T(8,128)(2,1)} collective-permute-done((bf16[1,4,48,5504]{3,2,1,0:T(8,128)(2,1)S(1)}, bf16[1,4,48,5504]{3,2,1,0:T(8,128)(2,1)}, u32[]{:S(2)}, u32[]{:S(2)}) %collective-permute-start) | collective-permute-done | bytes 2113568 | tf_op jit(solution)/shard_map/ppermute | solution.py:39
  91.9 0.0 collective-permute-start.1
  91.9 1.7 gather_fusion
  93.7 0.1 broadcast_select_fusion.1
  93.8 14.7 %all_to_all.9 = bf16[4,96,1024]{2,1,0:T(8,128)(2,1)} all-to-all(bf16[4,96,1024]{2,1,0:T(8,128)(2,1)S(1)} %broadcast_select_fusion.1), channel_id=1, replica_groups=mesh['layer'=4,'col'=4,'row'=2] {'layer'}, dimensions={0} | all-to-all | bytes 1572864 | tf_op jit(solution)/shard_map/all_to_all | solution.py:28
  108.5 0.0 all-gather.3.cloned.1.call-update
  108.6 0.0 all-reduce.3.cloned.1.call-start
  108.6 32.5 %collective-permute-done.1 = bf16[1,4,48,5504]{3,2,1,0:T(8,128)(2,1)} collective-permute-done((bf16[1,4,48,5504]{3,2,1,0:T(8,128)(2,1)}, bf16[1,4,48,5504]{3,2,1,0:T(8,128)(2,1)}, u32[]{:S(2)}, u32[]{:S(2)}) %collective-permute-start.1) | collective-permute-done | bytes 2113568 | tf_op jit(solution)/shard_map/ppermute | solution.py:39
  141.1 0.0 collective-permute-start.2
  141.1 0.0 all-gather.3.cloned.1.call-done
  141.1 7.7 %fusion.18 = bf16[1,768,2048]{2,1,0:T(8,128)(2,1)} fusion(bf16[768,1024]{1,0:T(8,128)(2,1)} %bitcast.73, bf16[1,1024,2048]{2,1,0:T(8,128)(2,1)} %param.11), kind=kOutput, calls=%fused_computation.16 | convolution fusion | flops 3222798336 | bytes 8912896 | tf_op jit(solution)/shard_map/ltc,lcj->ltj/dot_general | solution.py:46
  148.9 0.0 all-reduce.3.cloned.1.call-update
  148.9 0.2 all-reduce.5.cloned.1.call-start
  149.1 73.7 %collective-permute-done.2 = bf16[1,4,48,5504]{3,2,1,0:T(8,128)(2,1)} collective-permute-done((bf16[1,4,48,5504]{3,2,1,0:T(8,128)(2,1)}, bf16[1,4,48,5504]{3,2,1,0:T(8,128)(2,1)}, u32[]{:S(2)}, u32[]{:S(2)}) %collective-permute-start.2) | collective-permute-done | bytes 2113568 | tf_op jit(solution)/shard_map/ppermute | solution.py:39
  222.8 3.0 constant_dynamic-update-slice_fusion.7
  225.8 3.1 constant_dynamic-update-slice_fusion.6
  228.9 3.0 constant_dynamic-update-slice_fusion.5
  231.9 1.4 constant_dynamic-update-slice_fusion.4
  233.3 3.0 constant_dynamic-update-slice_fusion.3
  236.3 3.1 constant_dynamic-update-slice_fusion.2
  239.4 3.0 constant_dynamic-update-slice_fusion.1
  242.5 1.5 constant_dynamic-update-slice_fusion
  244.0 9.3 %constant_dynamic-slice_fusion = bf16[1,4,192,5504]{3,2,1,0:T(8,128)(2,1)} fusion(bf16[1,4,384,5504]{3,2,1,0:T(8,128)(2,1)} %constant_dynamic-update-slice_fusion, s32[]{:T(128)S(6)} %select_n.32), kind=kLoop, calls=%fused_computation.42 | loop fusion | bytes 16908292 | tf_op jit(solution)/shard_map/jit(_roll_dynamic)/dynamic_slice | solution.py:40
  253.3 31.4 %fusion.8 = bf16[1,768,2752]{1,2,0:T(8,128)(2,1)} fusion(bf16[768,5504]{1,0:T(8,128)(2,1)} %bitcast.72, bf16[1,5504,2752]{1,2,0:T(8,128)(2,1)} %param.12), kind=kOutput, calls=%fused_computation.11 | convolution fusion | flops 23267917824 | bytes 42975232 | tf_op jit(solution)/shard_map/ltr,lri->lti/dot_general | solution.py:50
  284.6 0.0 copy-start.2
  284.6 0.0 all-reduce.5.cloned.1.call-update
  285.3 0.0 copy-done.2
  285.3 17.0 %add_bitcast_fusion = f32[2752,2048]{1,0:T(8,128)} fusion(f32[1,2752,2048]{2,1,0:T(8,128)} %param.13, f32[]{:T(128)} %bitcast.70), kind=kLoop, calls=%fused_computation.7 | loop fusion | flops 5636096 | bytes 45088772 | tf_op jit(solution)/shard_map/div | solution.py:67
  302.3 0.0 all-reduce.3.cloned.1.call-done
  302.3 4.1 fusion.21
  306.3 5.8 %copy.12 = f32[512,2048]{0,1:T(8,128)} copy(f32[512,2048]{1,0:T(8,128)} %fusion.21) | data formatting | bytes 8388608 | tf_op jit(solution)/shard_map/mul | solution.py:69
  312.1 1.3 slice_bitcast_fusion.6
  313.4 96.8 %all-reduce.5.cloned.1.call-done = bf16[1,768,2752]{1,2,0:T(8,128)(2,1)} async-done(((bf16[1,768,2752]{1,2,0:T(8,128)(2,1)}), bf16[1,768,2752]{1,2,0:T(8,128)(2,1)}) %all-reduce.5.cloned.1.call-update) | async-done | bytes 4227088 | tf_op jit(solution)/shard_map/psum | solution.py:53
  410.2 3.5 slice_bitcast_fusion.13
  413.8 0.0 copy-start.3
  413.8 0.0 copy-start.1
  413.8 41.4 %fusion.4 = f32[4,512]{1,0:T(4,128)S(1)} fusion(f32[512,2048]{0,1:T(8,128)} %copy.12, f32[2752,2048]{1,0:T(8,128)} %add_bitcast_fusion, bf16[1,768,2752]{1,2,0:T(8,128)(2,1)} %all-reduce.5.cloned.1.call-done, bf16[256,2048]{1,0:T(8,128)(2,1)S(1)} %slice_bitcast_fusion.6, bf16[4,256]{1,0:T(4,128)(2,1)S(1)} %fusion.28, ...), kind=kOutput, calls=%fused_computation.9 | convolution fusion | flops 34690039808 | bytes 32024576 | tf_op jit(solution)/shard_map/ui,qij->quj/dot_general | solution.py:68
  455.2 0.0 copy-done.3
  455.2 0.3 fusion.26
  455.5 39.3 %psum.23 = f32[4,16]{1,0:T(4,128)} all-reduce(f32[4,16]{1,0:T(4,128)S(1)} %fusion.26), channel_id=1, replica_groups=mesh['layer'=4,'col'=4,'row'=2] {'layer','col','row'}, use_global_device_ids=true, to_apply=%region_3.4 | all-reduce | flops 64 | bytes 512 | tf_op jit(solution)/shard_map/psum | solution.py:71
  494.8 0.0 copy-done.1
  (2 shorter events, 0.0 us)
Async XLA Ops:
  6.5 1.6 copy-start
  6.5 134.6 %all-gather.3.cloned.1.call-start = ((), (), s32[]{:S(2)}) async-start(), calls=%async_computation.4 | async-start | bytes 2359296 | tf_op jit(solution)/shard_map/all_gather | solution.py:30
  42.0 49.9 %collective-permute-start = (bf16[1,4,48,5504]{3,2,1,0:T(8,128)(2,1)S(1)}, bf16[1,4,48,5504]{3,2,1,0:T(8,128)(2,1)}, u32[]{:S(2)}, u32[]{:S(2)}) collective-permute-start(bf16[1,4,48,5504]{3,2,1,0:T(8,128)(2,1)S(1)} %bitcast.71), channel_id=1, source_target_pairs={{0,2},{2,4},{4,6},{6,0},{1,3},{3,5},{5,7},{7,1},{8,10},{10,12},{12... | collective-permute-start | bytes 6340616 | tf_op jit(solution)/shard_map/ppermute | solution.py:39
  91.9 49.2 %collective-permute-start.1 = (bf16[1,4,48,5504]{3,2,1,0:T(8,128)(2,1)}, bf16[1,4,48,5504]{3,2,1,0:T(8,128)(2,1)}, u32[]{:S(2)}, u32[]{:S(2)}) collective-permute-start(bf16[1,4,48,5504]{3,2,1,0:T(8,128)(2,1)} %collective-permute-done), channel_id=1, source_target_pairs={{0,2},{2,4},{4,6},{6,0},{1,3},{3,5},{5,7},{7,1},{8,10},{10,12},{12... | collective-permute-start | bytes 6340616 | tf_op jit(solution)/shard_map/ppermute | solution.py:39
  108.6 193.7 %all-reduce.3.cloned.1.call-start = ((), (), s32[]{:S(2)}) async-start(), calls=%async_computation.2 | async-start | bytes 6291456 | tf_op jit(solution)/shard_map/psum | solution.py:49
  141.1 81.6 %collective-permute-start.2 = (bf16[1,4,48,5504]{3,2,1,0:T(8,128)(2,1)}, bf16[1,4,48,5504]{3,2,1,0:T(8,128)(2,1)}, u32[]{:S(2)}, u32[]{:S(2)}) collective-permute-start(bf16[1,4,48,5504]{3,2,1,0:T(8,128)(2,1)} %collective-permute-done.1), channel_id=1, source_target_pairs={{0,2},{2,4},{4,6},{6,0},{1,3},{3,5},{5,7},{7,1},{8,10},{10,12},{12... | collective-permute-start | bytes 6340616 | tf_op jit(solution)/shard_map/ppermute | solution.py:39
  148.9 261.3 %all-reduce.5.cloned.1.call-start = ((), (), s32[]{:S(2)}) async-start(), calls=%async_computation.3 | async-start | bytes 8454144 | tf_op jit(solution)/shard_map/psum | solution.py:53
  284.6 0.7 copy-start.2
  413.8 41.5 %copy-start.3 = (s32[512]{0:T(512)S(1)}, s32[512]{0:T(512)}, u32[]{:S(2)}) copy-start(s32[512]{0:T(512)} %param.17) | copy-start | bytes 6148
  413.8 81.0 %copy-start.1 = (bf16[4,48,5504]{2,1,0:T(8,128)(2,1)S(1)}, bf16[4,48,5504]{2,1,0:T(8,128)(2,1)}, u32[]{:S(2)}) copy-start(bf16[4,48,5504]{2,1,0:T(8,128)(2,1)} %param.10) | copy-start | bytes 6340612
Sparse Core Ops, SparseCore 0:
  108.7 27.6 all-gather.2
  149.0 151.0 all-reduce.2
  302.6 107.6 all-reduce.4
